TPU v7x, 128 devices: a whole 4x4x4 slice. The times are simulated.
128 devices in a mesh: ep: 8 (over y, core), fs: 16 (over z, x).
Axes of the slice: x: 4, y: 4, z: 4, core: 2. Of those that a mesh axis runs over, the one named last changes fastest.
Arguments:
- grads: bfloat16 [8, 8, 256, 14336], P('ep', None, 'fs'), may hold values from -64 to 64
- counts: int32 [8, 8], replicated, may hold values from 16 to 2047
- weight: bfloat16 [8, 256, 14336], P('ep', 'fs'), may hold values from -3 to 3
- mom: float32 [8, 256, 14336], P('ep', 'fs'), may hold values from -64 to 64
- second: float32 [8, 256, 14336], P('ep', 'fs'), may hold values from 0.1 to 10
- in_weight: float32 [6, 32], replicated, may hold values from -2.5 to 2.5
- in_bias: float32 [32], replicated, may hold values from -3 to 3
- out_weight: float32 [32, 2], replicated, may hold values from -1 to 1
- out_bias: float32 [2], replicated, may hold values from -3 to 3
Outputs:
- new_weight: bfloat16 [8, 256, 14336], P('ep')
- new_mom: float32 [8, 256, 14336], P('ep', 'fs')
- new_second: float32 [8, 256, 14336], P('ep', 'fs')
All inputs are finite; a program needn't handle non-finite values.
Results may differ from a plain program's by a relative error of at most 0.0019.
Values may be sent and summed in bfloat16 or wider, within the bound.
A program may use at most 64 MiB of HBM per device.

v0:
```python
import jax
import jax.numpy as jnp
from jax import lax
from jax.sharding import PartitionSpec as P

MOMENTUM_DECAY = 0.9
SECOND_DECAY = 0.99
NORM_EPS = 1e-06
ROOT_EPS = 1e-08
STEP_SCALE = 0.2
EXP_SCALE = 0.5


def from_everyone(value, axis):
    copies = jnp.broadcast_to(value, (lax.axis_size(axis), *value.shape))
    return lax.all_to_all(copies, axis, split_axis=0, concat_axis=0, tiled=True)


def of_everyone(value, axis):
    return from_everyone(value, axis).sum(axis=0)


def in_one(arrays, axis):
    line, at, done = (jnp.concatenate([a.reshape(-1) for a in arrays]), 0, [])
    so_far = of_everyone(line, axis)
    for a in arrays:
        done.append(so_far[at : at + a.size].reshape(a.shape))
        at += a.size
    return tuple(done)


def learned_step(
    gradient,
    mom_next,
    second_next,
    weight,
    grad_norm,
    mom_norm,
    in_weight,
    in_bias,
    out_weight,
    out_bias,
):
    inv_root = lax.rsqrt(second_next + ROOT_EPS)
    features = jnp.stack(
        [
            gradient / grad_norm,
            mom_next / mom_norm,
            mom_next * inv_root,
            gradient * inv_root,
            weight.astype(jnp.float32),
            jnp.broadcast_to(jnp.log(mom_norm), gradient.shape),
        ]
    )
    hidden = jax.nn.relu(
        jnp.einsum("fh,fab->hab", in_weight, features, precision=lax.Precision.HIGHEST)
        + in_bias[:, None, None]
    )
    outputs = (
        jnp.einsum("hk,hab->kab", out_weight, hidden, precision=lax.Precision.HIGHEST)
        + out_bias[:, None, None]
    )
    update = STEP_SCALE * outputs[0] * jnp.exp(EXP_SCALE * outputs[1])
    return (weight.astype(jnp.float32) - update).astype(jnp.bfloat16)


def add_sources(arrived):
    return jnp.sum(arrived.astype(jnp.float32), axis=0)


def per_device(grads, counts, weight, mom, second, in_weight, in_bias, out_weight, out_bias):
    source = lax.axis_index("ep")
    counts_f = counts.astype(jnp.float32)
    totals = jnp.sum(counts_f, axis=0)
    share_row = lax.dynamic_index_in_dim(counts_f, source, 0, keepdims=False) / totals
    weighted = share_row[None, :, None, None] * grads.astype(jnp.float32)
    outgoing = weighted.astype(jnp.bfloat16)
    gradient = add_sources(lax.all_to_all(outgoing, "ep", split_axis=1, concat_axis=0, tiled=True))[
        0
    ]
    mom_here = mom[0]
    second_here = second[0]
    mom_next = MOMENTUM_DECAY * mom_here + (1.0 - MOMENTUM_DECAY) * gradient
    second_next = SECOND_DECAY * second_here + (1.0 - SECOND_DECAY) * gradient * gradient
    entries = gradient.shape[0] * gradient.shape[1] * lax.axis_size("fs")
    grad_sq, mom_sq = in_one((jnp.sum(gradient * gradient), jnp.sum(mom_next * mom_next)), "fs")
    grad_norm = jnp.sqrt(grad_sq / entries + NORM_EPS)
    mom_norm = jnp.sqrt(mom_sq / entries + NORM_EPS)
    width = gradient.shape[1]

    def block_step(items):
        grad_block, mom_block, second_block, weight_block = items
        return learned_step(
            grad_block,
            mom_block,
            second_block,
            weight_block,
            grad_norm,
            mom_norm,
            in_weight,
            in_bias,
            out_weight,
            out_bias,
        )

    blocks = lax.map(
        block_step,
        (
            gradient.reshape(-1, 2, width),
            mom_next.reshape(-1, 2, width),
            second_next.reshape(-1, 2, width),
            weight[0].reshape(-1, 2, width),
        ),
    )
    updated = blocks.reshape(gradient.shape)
    gathered = lax.all_gather(updated[None], "fs", axis=1, tiled=True)
    return (gathered, mom_next[None], second_next[None])


def solution(mesh):
    in_specs = (
        P("ep", None, "fs", None),
        P(),
        P("ep", "fs", None),
        P("ep", "fs", None),
        P("ep", "fs", None),
        P(),
        P(),
        P(),
        P(),
    )
    out_specs = (P("ep", None, None), P("ep", "fs", None), P("ep", "fs", None))
    return jax.shard_map(
        per_device, mesh=mesh, in_specs=in_specs, out_specs=out_specs, check_vma=False
    )
```

profile of v0, /device:TPU:1, one launch (start us, length us, event | category | flops | bytes accessed | tf_op | source)
XLA Modules:
  0.0 246.2 jit_solution(12678078749305325285)
XLA Ops:
  8.6 4.7 %multiply_convert_fusion = bf16[1,8,16,14336]{3,2,0,1:T(8,128)(2,1)} fusion(bf16[1,8,16,14336]{3,2,1,0:T(8,128)(2,1)} %param.11, f32[8]{0:T(128)S(1)} %bitcast_divide_fusion), kind=kLoop, calls=%fused_computation.22 | loop fusion | flops 5505024 | bytes 7340064 | tf_op jit(solution)/shard_map/convert_element_type | solution.py:77
  13.3 6.1 %all-to-all-start = ((bf16[1,8,16,14336]{3,2,0,1:T(8,128)(2,1)}), bf16[1,8,16,14336]{3,2,0,1:T(8,128)(2,1)}, u32[]{:S(2)}, u32[]{:S(2)}) async-start(bf16[1,8,16,14336]{3,2,0,1:T(8,128)(2,1)} %multiply_convert_fusion), calls=%async_computation | async-start | bytes 7340032 | tf_op jit(solution)/shard_map/all_to_all | solution.py:78
  19.7 42.8 %all-to-all-done = bf16[1,8,16,14336]{3,2,0,1:T(8,128)(2,1)} async-done(((bf16[1,8,16,14336]{3,2,0,1:T(8,128)(2,1)}), bf16[1,8,16,14336]{3,2,0,1:T(8,128)(2,1)}, u32[]{:S(2)}, u32[]{:S(2)}) %all-to-all-start) | async-done | bytes 3670048 | tf_op jit(solution)/shard_map/all_to_all | solution.py:78
  62.5 2.6 %convert_reduce_fusion = f32[16,14336]{1,0:T(8,128)S(1)} fusion(bf16[1,8,16,14336]{3,2,0,1:T(8,128)(2,1)} %all-to-all-done), kind=kLoop, calls=%fused_computation.21 | loop fusion | flops 3440640 | bytes 4587520 | tf_op jit(solution)/shard_map/reduce_sum | solution.py:68
  69.5 7.6 %all-to-all-start.1 = ((f32[16,1,2]{2,1,0:T(1,128)}), f32[16,1,2]{2,1,0:T(1,128)S(1)}, u32[]{:S(2)}, u32[]{:S(2)}) async-start(f32[16,1,2]{2,1,0:T(1,128)} %broadcast_in_dim.18), calls=%async_computation.1 | async-start | bytes 16384 | tf_op jit(solution)/shard_map/all_to_all | solution.py:16
  77.3 2.9 %fusion.10 = (f32[1,16,14336]{2,1,0:T(8,128)}, f32[1,16,14336]{2,1,0:T(8,128)}, f32[1,16,14336]{2,1,0:T(8,128)}, f32[1,16,14336]{2,1,0:T(8,128)S(1)}) fusion(f32[16,14336]{1,0:T(8,128)S(1)} %convert_reduce_fusion, f32[1,16,14336]{2,1,0:T(8,128)} %param.15, f32[1,16,14336]{2,1,0:T(8,128)S(1)} %copy-done), kind=kLoop, calls=%fused_computation.26 | loop fusion | flops 1605632 | bytes 6422528 | tf_op jit(solution)/shard_map/add | solution.py:84
  82.5 4.1 %fusion.9 = (f32[8,2,14336]{2,0,1:T(8,128)S(1)}, f32[8,2,14336]{2,0,1:T(8,128)}, f32[8,2,14336]{2,0,1:T(8,128)}) fusion(f32[8,2,14336]{2,1,0:T(2,128)S(1)} %mul.131, f32[8,2,14336]{2,1,0:T(2,128)} %reshape_squeeze.7, f32[8,2,14336]{2,1,0:T(2,128)S(1)} %mul.126), kind=kLoop, calls=%fused_computation.25 | loop fusion | flops 1146880 | bytes 5505024 | tf_op jit(solution)/shard_map/add | solution.py:84
  88.4 75.6 %while.11 = (s32[]{:T(128)}, bf16[8,2,14336]{2,1,0:T(2,128)(2,1)}, bf16[8,2,14336]{2,1,0:T(2,128)(2,1)S(1)}, f32[8,2,14336]{2,0,1:T(8,128)}, f32[]{:T(128)}, /*i...) while((s32[]{:T(128)}, bf16[8,2,14336]{2,1,0:T(2,128)(2,1)}, ...), condition=%wide.region_6.7_spmd, body=%wide.region_5.6_spmd.sunk | while | flops 90316800 | bytes 11298093 | solution.py:106
  91.6 3.2 %fusion.28 = f32[32,2,14336]{2,0,1:T(8,128)S(1)} fusion(f32[6,2,14336]{2,0,1:T(8,128)S(1)} %stack.4, f32[32]{0:T(128)S(1)} %get-tuple-element.350, f32[6,32]{1,0:T(8,128)S(1)} %get-tuple-element.349), kind=kOutput, calls=%fused_computation.2.clone.1 | convolution fusion | flops 67895296 | bytes 4359040 | tf_op jit(solution)/shard_map/while/body/eval_jaxpr/fh,fab->hab/dot_general | solution.py:56
  94.8 2.1 fusion.29
  101.1 3.2 %fusion.28 = f32[32,2,14336]{2,0,1:T(8,128)S(1)} fusion(f32[6,2,14336]{2,0,1:T(8,128)S(1)} %stack.4, f32[32]{0:T(128)S(1)} %get-tuple-element.350, f32[6,32]{1,0:T(8,128)S(1)} %get-tuple-element.349), kind=kOutput, calls=%fused_computation.2.clone.1 | convolution fusion | flops 67895296 | bytes 4359040 | tf_op jit(solution)/shard_map/while/body/eval_jaxpr/fh,fab->hab/dot_general | solution.py:56
  104.3 2.1 fusion.29
  110.5 3.2 %fusion.28 = f32[32,2,14336]{2,0,1:T(8,128)S(1)} fusion(f32[6,2,14336]{2,0,1:T(8,128)S(1)} %stack.4, f32[32]{0:T(128)S(1)} %get-tuple-element.350, f32[6,32]{1,0:T(8,128)S(1)} %get-tuple-element.349), kind=kOutput, calls=%fused_computation.2.clone.1 | convolution fusion | flops 67895296 | bytes 4359040 | tf_op jit(solution)/shard_map/while/body/eval_jaxpr/fh,fab->hab/dot_general | solution.py:56
  113.7 2.1 fusion.29
  120.0 3.2 %fusion.28 = f32[32,2,14336]{2,0,1:T(8,128)S(1)} fusion(f32[6,2,14336]{2,0,1:T(8,128)S(1)} %stack.4, f32[32]{0:T(128)S(1)} %get-tuple-element.350, f32[6,32]{1,0:T(8,128)S(1)} %get-tuple-element.349), kind=kOutput, calls=%fused_computation.2.clone.1 | convolution fusion | flops 67895296 | bytes 4359040 | tf_op jit(solution)/shard_map/while/body/eval_jaxpr/fh,fab->hab/dot_general | solution.py:56
  123.2 2.1 fusion.29
  129.4 3.2 %fusion.28 = f32[32,2,14336]{2,0,1:T(8,128)S(1)} fusion(f32[6,2,14336]{2,0,1:T(8,128)S(1)} %stack.4, f32[32]{0:T(128)S(1)} %get-tuple-element.350, f32[6,32]{1,0:T(8,128)S(1)} %get-tuple-element.349), kind=kOutput, calls=%fused_computation.2.clone.1 | convolution fusion | flops 67895296 | bytes 4359040 | tf_op jit(solution)/shard_map/while/body/eval_jaxpr/fh,fab->hab/dot_general | solution.py:56
  132.6 2.1 fusion.29
  138.9 3.2 %fusion.28 = f32[32,2,14336]{2,0,1:T(8,128)S(1)} fusion(f32[6,2,14336]{2,0,1:T(8,128)S(1)} %stack.4, f32[32]{0:T(128)S(1)} %get-tuple-element.350, f32[6,32]{1,0:T(8,128)S(1)} %get-tuple-element.349), kind=kOutput, calls=%fused_computation.2.clone.1 | convolution fusion | flops 67895296 | bytes 4359040 | tf_op jit(solution)/shard_map/while/body/eval_jaxpr/fh,fab->hab/dot_general | solution.py:56
  142.1 2.1 fusion.29
  148.3 3.2 %fusion.28 = f32[32,2,14336]{2,0,1:T(8,128)S(1)} fusion(f32[6,2,14336]{2,0,1:T(8,128)S(1)} %stack.4, f32[32]{0:T(128)S(1)} %get-tuple-element.350, f32[6,32]{1,0:T(8,128)S(1)} %get-tuple-element.349), kind=kOutput, calls=%fused_computation.2.clone.1 | convolution fusion | flops 67895296 | bytes 4359040 | tf_op jit(solution)/shard_map/while/body/eval_jaxpr/fh,fab->hab/dot_general | solution.py:56
  157.8 3.2 %fusion.28 = f32[32,2,14336]{2,0,1:T(8,128)S(1)} fusion(f32[6,2,14336]{2,0,1:T(8,128)S(1)} %stack.4, f32[32]{0:T(128)S(1)} %get-tuple-element.350, f32[6,32]{1,0:T(8,128)S(1)} %get-tuple-element.349), kind=kOutput, calls=%fused_computation.2.clone.1 | convolution fusion | flops 67895296 | bytes 4359040 | tf_op jit(solution)/shard_map/while/body/eval_jaxpr/fh,fab->hab/dot_general | solution.py:56
  166.0 66.5 %all-gather.2.cloned.1.call-done = bf16[1,256,14336]{2,1,0:T(8,128)(2,1)} async-done(((bf16[1,16,14336]{2,1,0:T(8,128)(2,1)}), bf16[1,256,14336]{2,1,0:T(8,128)(2,1)}) %all-gather.2.cloned.1.call-update) | async-done | bytes 7340048 | tf_op jit(solution)/shard_map/all_gather | solution.py:116
  232.5 6.9 %copy.86 = bf16[1,256,14336]{2,1,0:T(8,128)(2,1)} copy(bf16[1,256,14336]{2,1,0:T(8,128)(2,1)} %all-gather.2.cloned.1.call-done) | data formatting | bytes 14680064
  (87 shorter events, 48.4 us)
Async XLA Ops:
  13.2 6.1 %copy-start.1 = (bf16[1,16,14336]{2,1,0:T(8,128)(2,1)S(1)}, bf16[1,16,14336]{2,1,0:T(8,128)(2,1)}, u32[]{:S(2)}) copy-start(bf16[1,16,14336]{2,1,0:T(8,128)(2,1)} %param.13) | copy-start | bytes 1376260
  13.3 49.3 %all-to-all-start = ((bf16[1,8,16,14336]{3,2,0,1:T(8,128)(2,1)}), bf16[1,8,16,14336]{3,2,0,1:T(8,128)(2,1)}, u32[]{:S(2)}, u32[]{:S(2)}) async-start(bf16[1,8,16,14336]{3,2,0,1:T(8,128)(2,1)} %multiply_convert_fusion), calls=%async_computation | async-start | bytes 7340032 | tf_op jit(solution)/shard_map/all_to_all | solution.py:78
  19.3 47.3 %copy-start = (f32[1,16,14336]{2,1,0:T(8,128)S(1)}, f32[1,16,14336]{2,1,0:T(8,128)}, u32[]{:S(2)}) copy-start(f32[1,16,14336]{2,1,0:T(8,128)} %param.14) | copy-start | bytes 2752516
  69.5 17.1 %all-to-all-start.1 = ((f32[16,1,2]{2,1,0:T(1,128)}), f32[16,1,2]{2,1,0:T(1,128)S(1)}, u32[]{:S(2)}, u32[]{:S(2)}) async-start(f32[16,1,2]{2,1,0:T(1,128)} %broadcast_in_dim.18), calls=%async_computation.1 | async-start | bytes 16384 | tf_op jit(solution)/shard_map/all_to_all | solution.py:16
  77.1 155.4 %all-gather.2.cloned.1.call-start = ((), (), s32[]{:S(2)}) async-start(), calls=%async_computation.2 | async-start | bytes 7798784 | tf_op jit(solution)/shard_map/all_gather | solution.py:116
  81.9 6.5 %copy-start.2 = (f32[6,32]{1,0:T(8,128)S(1)}, f32[6,32]{1,0:T(8,128)}, u32[]{:S(2)}) copy-start(f32[6,32]{1,0:T(8,128)} %param.16) | copy-start | bytes 2308
  81.9 6.5 %copy-start.3 = (f32[32,2]{0,1:T(2,128)S(1)}, f32[32,2]{0,1:T(2,128)}, u32[]{:S(2)}) copy-start(f32[32,2]{0,1:T(2,128)} %param.18) | copy-start | bytes 772
  81.9 6.5 %copy-start.4 = (f32[32]{0:T(128)S(1)}, f32[32]{0:T(128)}, u32[]{:S(2)}) copy-start(f32[32]{0:T(128)} %param.17) | copy-start | bytes 388
  81.9 6.5 %copy-start.5 = (f32[2]{0:T(128)S(1)}, f32[2]{0:T(128)}, u32[]{:S(2)}) copy-start(f32[2]{0:T(128)} %param.19) | copy-start | bytes 28
Sparse Core Ops, SparseCore 0:
  166.1 66.3 all-gather.1
where the time goes:
time: 247 us; the launch traced here: 246 us
  waiting for transfers between devices  109 us (44%)
  matrix products  42 us (17%)
  other arithmetic  35.8 us (14%)
  local copies, waits for them, and re-layouts  29.4 us (12%)
  between operations  15.4 us (6%)
  starting transfers between devices  13.9 us (6%)
    all_gather x1, waiting for transfers between devices, per_device(): gathered = lax.all_gather(updated[None], 'fs', axis=1, tiled=True)  66.5 us
    all_to_all x1, waiting for transfers between devices, per_device(): lax.all_to_all(outgoing, 'ep', split_axis=1, concat_axis=0, tiled=True)  42.8 us
    dot_general x8, matrix products, learned_step(): jnp.einsum('fh,fab->hab', in_weight, features, precision=lax.Precision.HI...  25.6 us
    dot_general x8, matrix products, learned_step(): jnp.einsum('hk,hab->kab', out_weight, hidden, precision=lax.Precision.HIG...  16.4 us
    mul x8, other arithmetic, learned_step(): gradient * inv_root  14.7 us
    another operation x8, local copies, waits for them, and re-layouts, learned_step(): jnp.stack([gradient / grad_norm, mom_next / mom_norm, mom_next * inv_root...  8.98 us
    all_to_all x1, starting transfers between devices, from_everyone(): return lax.all_to_all(copies, axis, split_axis=0, concat_axis=0, tiled=True)  7.6 us
    unnamed x13, local copies, waits for them, and re-layouts  6.93 us
  transfers between devices with their start and end apart: 3, of which 2 were waited for; matrix products, arithmetic and copies ran while one was open for 4% of the time, Pallas kernels for 0%

commit v1 on v0

--- a/solution.py
+++ b/solution.py
@@ -9,6 +9,24 @@
 ROOT_EPS = 1e-08
 STEP_SCALE = 0.2
 EXP_SCALE = 0.5
+
+
+def collect(shard, axis, dim):
+    ways, here, step = (lax.axis_size(axis), lax.axis_index(axis), shard.shape[dim])
+    shape = [n * ways if d == dim else n for d, n in enumerate(shard.shape)]
+    full = lax.dynamic_update_slice_in_dim(
+        jnp.zeros(shape, shard.dtype), shard, here * step, axis=dim
+    )
+    going_up = going_down = shard
+    for far in range(1, ways // 2 + 1):
+        going_up = lax.ppermute(going_up, axis, [(d, (d + 1) % ways) for d in range(ways)])
+        full = lax.dynamic_update_slice_in_dim(full, going_up, (here - far) % ways * step, axis=dim)
+        if 2 * far < ways:
+            going_down = lax.ppermute(going_down, axis, [(d, (d - 1) % ways) for d in range(ways)])
+            full = lax.dynamic_update_slice_in_dim(
+                full, going_down, (here + far) % ways * step, axis=dim
+            )
+    return full
 
 
 def from_everyone(value, axis):
@@ -113,7 +131,7 @@
         ),
     )
     updated = blocks.reshape(gradient.shape)
-    gathered = lax.all_gather(updated[None], "fs", axis=1, tiled=True)
+    gathered = collect(updated[None], "fs", 1)
     return (gathered, mom_next[None], second_next[None])
 
 

time: 247 us -> 272 us (1.10)
  the two profiles are of different devices: /device:TPU:1 before, /device:TPU:0 now
where the time goes in v1:
time: 272 us; the launch traced here: 271 us
  waiting for transfers between devices  111 us (41%)
  starting transfers between devices  51.1 us (19%)
  matrix products  42 us (15%)
  other arithmetic  37.7 us (14%)
  local copies, waits for them, and re-layouts  26.2 us (10%)
    ppermute x8, waiting for transfers between devices, collect(): lax.ppermute(going_up, axis, [(d, (d + 1) % ways) for d in range(ways)])  63.9 us
    all_to_all x1, waiting for transfers between devices, per_device(): lax.all_to_all(outgoing, 'ep', split_axis=1, concat_axis=0, tiled=True)  43.5 us
    ppermute x7, starting transfers between devices, collect(): lax.ppermute(going_down, axis, [(d, (d - 1) % ways) for d in range(ways)])  38 us
    dot_general x8, matrix products, learned_step(): jnp.einsum('fh,fab->hab', in_weight, features, precision=lax.Precision.HI...  25.6 us
    mul x8, other arithmetic, learned_step(): gradient * inv_root  16.9 us
    dot_general x8, matrix products, learned_step(): jnp.einsum('hk,hab->kab', out_weight, hidden, precision=lax.Precision.HIG...  16.4 us
    another operation x8, local copies, waits for them, and re-layouts, learned_step(): jnp.stack([gradient / grad_norm, mom_next / mom_norm, mom_next * inv_root...  8.98 us
    all_to_all x1, starting transfers between devices, from_everyone(): return lax.all_to_all(copies, axis, split_axis=0, concat_axis=0, tiled=True)  7.89 us
  transfers between devices with their start and end apart: 17, of which 11 were waited for; matrix products, arithmetic and copies ran while one was open for 2% of the time, Pallas kernels for 0%

profile of v1, /device:TPU:0, one launch (start us, length us, event | category | flops | bytes accessed | tf_op | source)
XLA Modules:
  0.0 271.3 jit_solution(6175109779725905088)
XLA Ops:
  2.0 4.7 %multiply_convert_fusion = bf16[1,8,16,14336]{3,2,0,1:T(8,128)(2,1)} fusion(bf16[1,8,16,14336]{3,2,1,0:T(8,128)(2,1)} %param.11, f32[8]{0:T(128)S(1)} %fusion.15), kind=kLoop, calls=%fused_computation.22 | loop fusion | flops 5505024 | bytes 7340064 | tf_op jit(solution)/shard_map/convert_element_type | solution.py:95
  6.8 4.7 %all-to-all-start = ((bf16[1,8,16,14336]{3,2,0,1:T(8,128)(2,1)}), bf16[1,8,16,14336]{3,2,0,1:T(8,128)(2,1)}, u32[]{:S(2)}, u32[]{:S(2)}) async-start(bf16[1,8,16,14336]{3,2,0,1:T(8,128)(2,1)} %multiply_convert_fusion), calls=%async_computation | async-start | bytes 7340032 | tf_op jit(solution)/shard_map/all_to_all | solution.py:96
  12.1 43.5 %all-to-all-done = bf16[1,8,16,14336]{3,2,0,1:T(8,128)(2,1)} async-done(((bf16[1,8,16,14336]{3,2,0,1:T(8,128)(2,1)}), bf16[1,8,16,14336]{3,2,0,1:T(8,128)(2,1)}, u32[]{:S(2)}, u32[]{:S(2)}) %all-to-all-start) | async-done | bytes 3670048 | tf_op jit(solution)/shard_map/all_to_all | solution.py:96
  67.7 7.9 %all-to-all-start.1 = ((f32[16,1,2]{2,1,0:T(1,128)}), f32[16,1,2]{2,1,0:T(1,128)S(1)}, u32[]{:S(2)}, u32[]{:S(2)}) async-start(f32[16,1,2]{2,1,0:T(1,128)} %broadcast_in_dim.22), calls=%async_computation.1 | async-start | bytes 16384 | tf_op jit(solution)/shard_map/all_to_all | solution.py:34
  75.6 3.8 %fusion.9 = (f32[8,2,14336]{2,0,1:T(8,128)}, f32[8,2,14336]{2,0,1:T(8,128)}, f32[8,2,14336]{2,0,1:T(8,128)}) fusion(f32[8,2,14336]{2,1,0:T(2,128)S(1)} %mul.179, f32[8,2,14336]{2,1,0:T(2,128)} %reshape_squeeze.7, f32[8,2,14336]{2,1,0:T(2,128)S(1)} %mul.174), kind=kLoop, calls=%fused_computation.25 | loop fusion | flops 1146880 | bytes 5505024 | tf_op jit(solution)/shard_map/add | solution.py:102
  79.4 3.8 %all-to-all-done.1 = f32[16,1,2]{2,1,0:T(1,128)S(1)} async-done(((f32[16,1,2]{2,1,0:T(1,128)}), f32[16,1,2]{2,1,0:T(1,128)S(1)}, u32[]{:S(2)}, u32[]{:S(2)}) %all-to-all-start.1) | async-done | bytes 160 | tf_op jit(solution)/shard_map/all_to_all | solution.py:34
  85.2 77.8 %while.11 = (s32[]{:T(128)}, bf16[8,2,14336]{2,1,0:T(2,128)(2,1)}, bf16[8,2,14336]{2,1,0:T(2,128)(2,1)S(1)}, f32[8,2,14336]{2,0,1:T(8,128)}, f32[]{:T(128)}, /*i...) while((s32[]{:T(128)}, bf16[8,2,14336]{2,1,0:T(2,128)(2,1)}, ...), condition=%wide.region_6.7_spmd, body=%wide.region_5.6_spmd.sunk | while | flops 90316800 | bytes 11298593 | solution.py:124
  137.3 3.2 %fusion.30 = f32[32,2,14336]{2,0,1:T(8,128)S(1)} fusion(f32[6,2,14336]{2,0,1:T(8,128)S(1)} %stack.4, f32[32]{0:T(128)S(1)} %get-tuple-element.350, f32[6,32]{1,0:T(8,128)S(1)} %get-tuple-element.349), kind=kOutput, calls=%fused_computation.2.clone.1 | convolution fusion | flops 67895296 | bytes 4359040 | tf_op jit(solution)/shard_map/while/body/eval_jaxpr/fh,fab->hab/dot_general | solution.py:74
  147.0 3.2 %fusion.30 = f32[32,2,14336]{2,0,1:T(8,128)S(1)} fusion(f32[6,2,14336]{2,0,1:T(8,128)S(1)} %stack.4, f32[32]{0:T(128)S(1)} %get-tuple-element.350, f32[6,32]{1,0:T(8,128)S(1)} %get-tuple-element.349), kind=kOutput, calls=%fused_computation.2.clone.1 | convolution fusion | flops 67895296 | bytes 4359040 | tf_op jit(solution)/shard_map/while/body/eval_jaxpr/fh,fab->hab/dot_general | solution.py:74
  164.7 4.9 %collective-permute-start.1 = (bf16[1,16,14336]{2,1,0:T(8,128)(2,1)S(1)}, bf16[1,16,14336]{2,1,0:T(8,128)(2,1)S(1)}, u32[]{:S(2)}, u32[]{:S(2)}) collective-permute-start(bf16[1,16,14336]{2,1,0:T(8,128)(2,1)S(1)} %broadcast_in_dim_reshape.3), channel_id=1, source_target_pairs={{0,15},{1,0},{2,1},{3,2},{4,3},{5,4},{6,5},{7,6},{8,7},{9,8},{10,9... | collective-permute-start | bytes 1376264 | tf_op jit(solution)/shard_map/ppermute | solution.py:25
  170.5 7.5 %collective-permute-done = bf16[1,16,14336]{2,1,0:T(8,128)(2,1)S(1)} collective-permute-done((bf16[1,16,14336]{2,1,0:T(8,128)(2,1)S(1)}, bf16[1,16,14336]{2,1,0:T(8,128)(2,1)S(1)}, u32[]{:S(2)}, u32[]{:S(2)}) %collective-permute-start) | collective-permute-done | bytes 458784 | tf_op jit(solution)/shard_map/ppermute | solution.py:22
  178.0 5.3 %collective-permute-start.3 = (bf16[1,16,14336]{2,1,0:T(8,128)(2,1)S(1)}, bf16[1,16,14336]{2,1,0:T(8,128)(2,1)S(1)}, u32[]{:S(2)}, u32[]{:S(2)}) collective-permute-start(bf16[1,16,14336]{2,1,0:T(8,128)(2,1)S(1)} %collective-permute-done.1), channel_id=1, source_target_pairs={{0,15},{1,0},{2,1},{3,2},{4,3},{5,4},{6,5},{7,6},{8,7},{9,8},{10,9... | collective-permute-start | bytes 1376264 | tf_op jit(solution)/shard_map/ppermute | solution.py:25
  183.4 7.4 %collective-permute-done.2 = bf16[1,16,14336]{2,1,0:T(8,128)(2,1)S(1)} collective-permute-done((bf16[1,16,14336]{2,1,0:T(8,128)(2,1)S(1)}, bf16[1,16,14336]{2,1,0:T(8,128)(2,1)S(1)}, u32[]{:S(2)}, u32[]{:S(2)}) %collective-permute-start.2) | collective-permute-done | bytes 458784 | tf_op jit(solution)/shard_map/ppermute | solution.py:22
  190.8 5.3 %collective-permute-start.5 = (bf16[1,16,14336]{2,1,0:T(8,128)(2,1)S(1)}, bf16[1,16,14336]{2,1,0:T(8,128)(2,1)S(1)}, u32[]{:S(2)}, u32[]{:S(2)}) collective-permute-start(bf16[1,16,14336]{2,1,0:T(8,128)(2,1)S(1)} %collective-permute-done.3), channel_id=1, source_target_pairs={{0,15},{1,0},{2,1},{3,2},{4,3},{5,4},{6,5},{7,6},{8,7},{9,8},{10,9... | collective-permute-start | bytes 1376264 | tf_op jit(solution)/shard_map/ppermute | solution.py:25
  196.3 6.6 %collective-permute-done.4 = bf16[1,16,14336]{2,1,0:T(8,128)(2,1)S(1)} collective-permute-done((bf16[1,16,14336]{2,1,0:T(8,128)(2,1)S(1)}, bf16[1,16,14336]{2,1,0:T(8,128)(2,1)S(1)}, u32[]{:S(2)}, u32[]{:S(2)}) %collective-permute-start.4) | collective-permute-done | bytes 458784 | tf_op jit(solution)/shard_map/ppermute | solution.py:22
  202.8 5.3 %collective-permute-start.7 = (bf16[1,16,14336]{2,1,0:T(8,128)(2,1)S(1)}, bf16[1,16,14336]{2,1,0:T(8,128)(2,1)S(1)}, u32[]{:S(2)}, u32[]{:S(2)}) collective-permute-start(bf16[1,16,14336]{2,1,0:T(8,128)(2,1)S(1)} %collective-permute-done.5), channel_id=1, source_target_pairs={{0,15},{1,0},{2,1},{3,2},{4,3},{5,4},{6,5},{7,6},{8,7},{9,8},{10,9... | collective-permute-start | bytes 1376264 | tf_op jit(solution)/shard_map/ppermute | solution.py:25
  208.3 6.4 %collective-permute-done.6 = bf16[1,16,14336]{2,1,0:T(8,128)(2,1)S(1)} collective-permute-done((bf16[1,16,14336]{2,1,0:T(8,128)(2,1)S(1)}, bf16[1,16,14336]{2,1,0:T(8,128)(2,1)S(1)}, u32[]{:S(2)}, u32[]{:S(2)}) %collective-permute-start.6) | collective-permute-done | bytes 458784 | tf_op jit(solution)/shard_map/ppermute | solution.py:22
  214.6 5.5 %collective-permute-start.9 = (bf16[1,16,14336]{2,1,0:T(8,128)(2,1)S(1)}, bf16[1,16,14336]{2,1,0:T(8,128)(2,1)S(1)}, u32[]{:S(2)}, u32[]{:S(2)}) collective-permute-start(bf16[1,16,14336]{2,1,0:T(8,128)(2,1)S(1)} %collective-permute-done.7), channel_id=1, source_target_pairs={{0,15},{1,0},{2,1},{3,2},{4,3},{5,4},{6,5},{7,6},{8,7},{9,8},{10,9... | collective-permute-start | bytes 1376264 | tf_op jit(solution)/shard_map/ppermute | solution.py:25
  220.2 7.2 %collective-permute-done.8 = bf16[1,16,14336]{2,1,0:T(8,128)(2,1)S(1)} collective-permute-done((bf16[1,16,14336]{2,1,0:T(8,128)(2,1)S(1)}, bf16[1,16,14336]{2,1,0:T(8,128)(2,1)S(1)}, u32[]{:S(2)}, u32[]{:S(2)}) %collective-permute-start.8) | collective-permute-done | bytes 458784 | tf_op jit(solution)/shard_map/ppermute | solution.py:22
  227.4 5.7 %collective-permute-start.11 = (bf16[1,16,14336]{2,1,0:T(8,128)(2,1)S(1)}, bf16[1,16,14336]{2,1,0:T(8,128)(2,1)S(1)}, u32[]{:S(2)}, u32[]{:S(2)}) collective-permute-start(bf16[1,16,14336]{2,1,0:T(8,128)(2,1)S(1)} %collective-permute-done.9), channel_id=1, source_target_pairs={{0,15},{1,0},{2,1},{3,2},{4,3},{5,4},{6,5},{7,6},{8,7},{9,8},{10,9... | collective-permute-start | bytes 1376264 | tf_op jit(solution)/shard_map/ppermute | solution.py:25
  233.2 8.1 %collective-permute-done.10 = bf16[1,16,14336]{2,1,0:T(8,128)(2,1)S(1)} collective-permute-done((bf16[1,16,14336]{2,1,0:T(8,128)(2,1)S(1)}, bf16[1,16,14336]{2,1,0:T(8,128)(2,1)S(1)}, u32[]{:S(2)}, u32[]{:S(2)}) %collective-permute-start.10) | collective-permute-done | bytes 458784 | tf_op jit(solution)/shard_map/ppermute | solution.py:22
  241.6 5.8 %collective-permute-start.13 = (bf16[1,16,14336]{2,1,0:T(8,128)(2,1)S(1)}, bf16[1,16,14336]{2,1,0:T(8,128)(2,1)S(1)}, u32[]{:S(2)}, u32[]{:S(2)}) collective-permute-start(bf16[1,16,14336]{2,1,0:T(8,128)(2,1)S(1)} %collective-permute-done.11), channel_id=1, source_target_pairs={{0,15},{1,0},{2,1},{3,2},{4,3},{5,4},{6,5},{7,6},{8,7},{9,8},{10,9... | collective-permute-start | bytes 1376264 | tf_op jit(solution)/shard_map/ppermute | solution.py:25
  247.4 9.0 %collective-permute-done.12 = bf16[1,16,14336]{2,1,0:T(8,128)(2,1)S(1)} collective-permute-done((bf16[1,16,14336]{2,1,0:T(8,128)(2,1)S(1)}, bf16[1,16,14336]{2,1,0:T(8,128)(2,1)S(1)}, u32[]{:S(2)}, u32[]{:S(2)}) %collective-permute-start.12) | collective-permute-done | bytes 458784 | tf_op jit(solution)/shard_map/ppermute | solution.py:22
  256.5 11.7 %collective-permute-done.14 = bf16[1,16,14336]{2,1,0:T(8,128)(2,1)S(1)} collective-permute-done((bf16[1,16,14336]{2,1,0:T(8,128)(2,1)S(1)}, bf16[1,16,14336]{2,1,0:T(8,128)(2,1)S(1)}, u32[]{:S(2)}, u32[]{:S(2)}) %collective-permute-start.14) | collective-permute-done | bytes 458784 | tf_op jit(solution)/shard_map/ppermute | solution.py:22
  (132 shorter events, 91.8 us)
Async XLA Ops:
  2.0 9.7 %copy-start.2 = (bf16[1,16,14336]{2,1,0:T(8,128)(2,1)S(1)}, bf16[1,16,14336]{2,1,0:T(8,128)(2,1)}, u32[]{:S(2)}) copy-start(bf16[1,16,14336]{2,1,0:T(8,128)(2,1)} %param.13) | copy-start | bytes 1376260
  6.8 52.9 %copy-start.1 = (f32[1,16,14336]{2,1,0:T(8,128)S(1)}, f32[1,16,14336]{2,1,0:T(8,128)}, u32[]{:S(2)}) copy-start(f32[1,16,14336]{2,1,0:T(8,128)} %param.14) | copy-start | bytes 2752516
  6.8 48.8 %all-to-all-start = ((bf16[1,8,16,14336]{3,2,0,1:T(8,128)(2,1)}), bf16[1,8,16,14336]{3,2,0,1:T(8,128)(2,1)}, u32[]{:S(2)}, u32[]{:S(2)}) async-start(bf16[1,8,16,14336]{3,2,0,1:T(8,128)(2,1)} %multiply_convert_fusion), calls=%async_computation | async-start | bytes 7340032 | tf_op jit(solution)/shard_map/all_to_all | solution.py:96
  60.6 24.5 %copy-start.3 = (f32[6,32]{1,0:T(8,128)S(1)}, f32[6,32]{1,0:T(8,128)}, u32[]{:S(2)}) copy-start(f32[6,32]{1,0:T(8,128)} %param.16) | copy-start | bytes 2308
  60.7 24.5 %copy-start.4 = (f32[32,2]{0,1:T(2,128)S(1)}, f32[32,2]{0,1:T(2,128)}, u32[]{:S(2)}) copy-start(f32[32,2]{0,1:T(2,128)} %param.18) | copy-start | bytes 772
  60.7 24.5 %copy-start.5 = (f32[32]{0:T(128)S(1)}, f32[32]{0:T(128)}, u32[]{:S(2)}) copy-start(f32[32]{0:T(128)} %param.17) | copy-start | bytes 388
  60.7 24.5 %copy-start.6 = (f32[2]{0:T(128)S(1)}, f32[2]{0:T(128)}, u32[]{:S(2)}) copy-start(f32[2]{0:T(128)} %param.19) | copy-start | bytes 28
  67.7 15.5 %all-to-all-start.1 = ((f32[16,1,2]{2,1,0:T(1,128)}), f32[16,1,2]{2,1,0:T(1,128)S(1)}, u32[]{:S(2)}, u32[]{:S(2)}) async-start(f32[16,1,2]{2,1,0:T(1,128)} %broadcast_in_dim.22), calls=%async_computation.1 | async-start | bytes 16384 | tf_op jit(solution)/shard_map/all_to_all | solution.py:34
  164.2 13.8 %collective-permute-start = (bf16[1,16,14336]{2,1,0:T(8,128)(2,1)S(1)}, bf16[1,16,14336]{2,1,0:T(8,128)(2,1)S(1)}, u32[]{:S(2)}, u32[]{:S(2)}) collective-permute-start(bf16[1,16,14336]{2,1,0:T(8,128)(2,1)S(1)} %broadcast_in_dim_reshape.3), channel_id=1, source_target_pairs={{0,1},{1,2},{2,3},{3,4},{4,5},{5,6},{6,7},{7,8},{8,9},{9,10},{10,1... | collective-permute-start | bytes 1376264 | tf_op jit(solution)/shard_map/ppermute | solution.py:22
  164.7 13.3 %collective-permute-start.1 = (bf16[1,16,14336]{2,1,0:T(8,128)(2,1)S(1)}, bf16[1,16,14336]{2,1,0:T(8,128)(2,1)S(1)}, u32[]{:S(2)}, u32[]{:S(2)}) collective-permute-start(bf16[1,16,14336]{2,1,0:T(8,128)(2,1)S(1)} %broadcast_in_dim_reshape.3), channel_id=1, source_target_pairs={{0,15},{1,0},{2,1},{3,2},{4,3},{5,4},{6,5},{7,6},{8,7},{9,8},{10,9... | collective-permute-start | bytes 1376264 | tf_op jit(solution)/shard_map/ppermute | solution.py:25
  178.0 12.9 %collective-permute-start.2 = (bf16[1,16,14336]{2,1,0:T(8,128)(2,1)S(1)}, bf16[1,16,14336]{2,1,0:T(8,128)(2,1)S(1)}, u32[]{:S(2)}, u32[]{:S(2)}) collective-permute-start(bf16[1,16,14336]{2,1,0:T(8,128)(2,1)S(1)} %collective-permute-done), channel_id=1, source_target_pairs={{0,1},{1,2},{2,3},{3,4},{4,5},{5,6},{6,7},{7,8},{8,9},{9,10},{10,1... | collective-permute-start | bytes 1376264 | tf_op jit(solution)/shard_map/ppermute | solution.py:22
  178.0 12.9 %collective-permute-start.3 = (bf16[1,16,14336]{2,1,0:T(8,128)(2,1)S(1)}, bf16[1,16,14336]{2,1,0:T(8,128)(2,1)S(1)}, u32[]{:S(2)}, u32[]{:S(2)}) collective-permute-start(bf16[1,16,14336]{2,1,0:T(8,128)(2,1)S(1)} %collective-permute-done.1), channel_id=1, source_target_pairs={{0,15},{1,0},{2,1},{3,2},{4,3},{5,4},{6,5},{7,6},{8,7},{9,8},{10,9... | collective-permute-start | bytes 1376264 | tf_op jit(solution)/shard_map/ppermute | solution.py:25
  190.8 12.0 %collective-permute-start.4 = (bf16[1,16,14336]{2,1,0:T(8,128)(2,1)S(1)}, bf16[1,16,14336]{2,1,0:T(8,128)(2,1)S(1)}, u32[]{:S(2)}, u32[]{:S(2)}) collective-permute-start(bf16[1,16,14336]{2,1,0:T(8,128)(2,1)S(1)} %collective-permute-done.2), channel_id=1, source_target_pairs={{0,1},{1,2},{2,3},{3,4},{4,5},{5,6},{6,7},{7,8},{8,9},{9,10},{10,1... | collective-permute-start | bytes 1376264 | tf_op jit(solution)/shard_map/ppermute | solution.py:22
  190.8 12.0 %collective-permute-start.5 = (bf16[1,16,14336]{2,1,0:T(8,128)(2,1)S(1)}, bf16[1,16,14336]{2,1,0:T(8,128)(2,1)S(1)}, u32[]{:S(2)}, u32[]{:S(2)}) collective-permute-start(bf16[1,16,14336]{2,1,0:T(8,128)(2,1)S(1)} %collective-permute-done.3), channel_id=1, source_target_pairs={{0,15},{1,0},{2,1},{3,2},{4,3},{5,4},{6,5},{7,6},{8,7},{9,8},{10,9... | collective-permute-start | bytes 1376264 | tf_op jit(solution)/shard_map/ppermute | solution.py:25
  202.8 11.8 %collective-permute-start.6 = (bf16[1,16,14336]{2,1,0:T(8,128)(2,1)S(1)}, bf16[1,16,14336]{2,1,0:T(8,128)(2,1)S(1)}, u32[]{:S(2)}, u32[]{:S(2)}) collective-permute-start(bf16[1,16,14336]{2,1,0:T(8,128)(2,1)S(1)} %collective-permute-done.4), channel_id=1, source_target_pairs={{0,1},{1,2},{2,3},{3,4},{4,5},{5,6},{6,7},{7,8},{8,9},{9,10},{10,1... | collective-permute-start | bytes 1376264 | tf_op jit(solution)/shard_map/ppermute | solution.py:22
  202.8 11.8 %collective-permute-start.7 = (bf16[1,16,14336]{2,1,0:T(8,128)(2,1)S(1)}, bf16[1,16,14336]{2,1,0:T(8,128)(2,1)S(1)}, u32[]{:S(2)}, u32[]{:S(2)}) collective-permute-start(bf16[1,16,14336]{2,1,0:T(8,128)(2,1)S(1)} %collective-permute-done.5), channel_id=1, source_target_pairs={{0,15},{1,0},{2,1},{3,2},{4,3},{5,4},{6,5},{7,6},{8,7},{9,8},{10,9... | collective-permute-start | bytes 1376264 | tf_op jit(solution)/shard_map/ppermute | solution.py:25
  214.6 12.8 %collective-permute-start.8 = (bf16[1,16,14336]{2,1,0:T(8,128)(2,1)S(1)}, bf16[1,16,14336]{2,1,0:T(8,128)(2,1)S(1)}, u32[]{:S(2)}, u32[]{:S(2)}) collective-permute-start(bf16[1,16,14336]{2,1,0:T(8,128)(2,1)S(1)} %collective-permute-done.6), channel_id=1, source_target_pairs={{0,1},{1,2},{2,3},{3,4},{4,5},{5,6},{6,7},{7,8},{8,9},{9,10},{10,1... | collective-permute-start | bytes 1376264 | tf_op jit(solution)/shard_map/ppermute | solution.py:22
  214.6 12.8 %collective-permute-start.9 = (bf16[1,16,14336]{2,1,0:T(8,128)(2,1)S(1)}, bf16[1,16,14336]{2,1,0:T(8,128)(2,1)S(1)}, u32[]{:S(2)}, u32[]{:S(2)}) collective-permute-start(bf16[1,16,14336]{2,1,0:T(8,128)(2,1)S(1)} %collective-permute-done.7), channel_id=1, source_target_pairs={{0,15},{1,0},{2,1},{3,2},{4,3},{5,4},{6,5},{7,6},{8,7},{9,8},{10,9... | collective-permute-start | bytes 1376264 | tf_op jit(solution)/shard_map/ppermute | solution.py:25
  227.4 13.9 %collective-permute-start.10 = (bf16[1,16,14336]{2,1,0:T(8,128)(2,1)S(1)}, bf16[1,16,14336]{2,1,0:T(8,128)(2,1)S(1)}, u32[]{:S(2)}, u32[]{:S(2)}) collective-permute-start(bf16[1,16,14336]{2,1,0:T(8,128)(2,1)S(1)} %collective-permute-done.8), channel_id=1, source_target_pairs={{0,1},{1,2},{2,3},{3,4},{4,5},{5,6},{6,7},{7,8},{8,9},{9,10},{10,1... | collective-permute-start | bytes 1376264 | tf_op jit(solution)/shard_map/ppermute | solution.py:22
  227.4 14.1 %collective-permute-start.11 = (bf16[1,16,14336]{2,1,0:T(8,128)(2,1)S(1)}, bf16[1,16,14336]{2,1,0:T(8,128)(2,1)S(1)}, u32[]{:S(2)}, u32[]{:S(2)}) collective-permute-start(bf16[1,16,14336]{2,1,0:T(8,128)(2,1)S(1)} %collective-permute-done.9), channel_id=1, source_target_pairs={{0,15},{1,0},{2,1},{3,2},{4,3},{5,4},{6,5},{7,6},{8,7},{9,8},{10,9... | collective-permute-start | bytes 1376264 | tf_op jit(solution)/shard_map/ppermute | solution.py:25
  241.3 15.1 %collective-permute-start.12 = (bf16[1,16,14336]{2,1,0:T(8,128)(2,1)S(1)}, bf16[1,16,14336]{2,1,0:T(8,128)(2,1)S(1)}, u32[]{:S(2)}, u32[]{:S(2)}) collective-permute-start(bf16[1,16,14336]{2,1,0:T(8,128)(2,1)S(1)} %collective-permute-done.10), channel_id=1, source_target_pairs={{0,1},{1,2},{2,3},{3,4},{4,5},{5,6},{6,7},{7,8},{8,9},{9,10},{10,1... | collective-permute-start | bytes 1376264 | tf_op jit(solution)/shard_map/ppermute | solution.py:22
  241.6 14.9 %collective-permute-start.13 = (bf16[1,16,14336]{2,1,0:T(8,128)(2,1)S(1)}, bf16[1,16,14336]{2,1,0:T(8,128)(2,1)S(1)}, u32[]{:S(2)}, u32[]{:S(2)}) collective-permute-start(bf16[1,16,14336]{2,1,0:T(8,128)(2,1)S(1)} %collective-permute-done.11), channel_id=1, source_target_pairs={{0,15},{1,0},{2,1},{3,2},{4,3},{5,4},{6,5},{7,6},{8,7},{9,8},{10,9... | collective-permute-start | bytes 1376264 | tf_op jit(solution)/shard_map/ppermute | solution.py:25
  256.4 11.8 %collective-permute-start.14 = (bf16[1,16,14336]{2,1,0:T(8,128)(2,1)S(1)}, bf16[1,16,14336]{2,1,0:T(8,128)(2,1)S(1)}, u32[]{:S(2)}, u32[]{:S(2)}) collective-permute-start(bf16[1,16,14336]{2,1,0:T(8,128)(2,1)S(1)} %collective-permute-done.12), channel_id=1, source_target_pairs={{0,1},{1,2},{2,3},{3,4},{4,5},{5,6},{6,7},{7,8},{8,9},{9,10},{10,1... | collective-permute-start | bytes 1376264 | tf_op jit(solution)/shard_map/ppermute | solution.py:22
  268.3 3.1 %copy-start = (bf16[1,256,14336]{2,1,0:T(8,128)(2,1)}, bf16[1,256,14336]{2,1,0:T(8,128)(2,1)S(1)}, u32[]{:S(2)}) copy-start(bf16[1,256,14336]{2,1,0:T(8,128)(2,1)S(1)} %constant_dynamic-update-slice_fusion) | copy-start | bytes 22020100
